TPU v7x, 256 devices: a whole 4x4x8 slice. The times are simulated.
256 devices in a mesh: enc: 8 (over z), bin: 16 (over y_hi, x, core), off: 2 (over y_lo).
Axes of the slice: x: 4, y: 4 (y_hi: 2, y_lo: 2; y = y_hi * 2 + y_lo), z: 8, core: 2. Of those that a mesh axis runs over, the one named last changes fastest.
Arguments:
- encoder_in: bfloat16 [512, 6144], P(('bin', 'off'), 'enc'), may hold values from -6 to 6
- gain_enc: float32 [512], P(('bin', 'off')), may hold values from 0.1 to 1.9
- conv_one: bfloat16 [3, 512, 512], P(None, ('bin', 'off')), may hold values from -0.15625 to 0.15625
- proj_weight: bfloat16 [2, 512, 32], P(None, ('bin', 'off')), may hold values from -0.25 to 0.25
- conv_two: bfloat16 [9, 32, 32], replicated, may hold values from -0.375 to 0.375
- head_weight: float32 [32], replicated, may hold values from -1 to 1
- target: bfloat16 [6144, 2048], P('bin', ('enc', 'off')), may hold values from -8 to 8
- valid_bins: int32 [6144], replicated, may hold values 0 or 1
- offset_limit: int32 [6144], replicated, may hold values from 1024 to 2048
- dilations: int32 [2], replicated, may hold values from 1 to 8, as said below
Outputs:
- prediction: float32 [6144, 2048], P('bin', ('enc', 'off'))
- loss_mean: float32 [1], replicated
- grad_conv_two: float32 [9, 32, 32], replicated
- grad_proj: float32 [2, 512, 32], P(None, ('bin', 'off'))
- grad_conv_one: float32 [3, 512, 512], P(None, ('bin', 'off'), 'enc')
Inputs may be any that keep to these rules, and one draw needn't show every extreme that they name: dilations[0] is the dilation of the 1-D layer and dilations[1] that of the 2-D layer; one of the two equals 8, the other is smaller.
All inputs are finite; a program needn't handle non-finite values.
Results may differ from a plain program's by a relative error of at most 0.0013.
The roundings to bfloat16 on the way count: a program that leaves them out, or rounds other values in their place, can miss the bound.
Values may be sent and summed in bfloat16 or wider, within the bound.
No kernel may reach another device: no remote copies, remote signals or barrier semaphores. Data moves between devices by JAX's collectives and lax.ppermute only.
A program may use at most 192 MiB of HBM per device.

v0:
```python
import jax
import jax.numpy as jnp
from jax import lax
from jax.sharding import PartitionSpec as P

LARGEST_DILATION = 8


def with_halo(cells, sides, width):
    for axis, dim in sides:
        count = lax.axis_size(axis)
        ends = count - 1
        head = lax.slice_in_dim(cells, 0, width, axis=dim)
        tail = lax.slice_in_dim(cells, cells.shape[dim] - width, cells.shape[dim], axis=dim)
        cells = jnp.concatenate(
            [
                lax.ppermute(tail, axis, [(i, (i + 1) % count) for i in range(ends)]),
                cells,
                lax.ppermute(head, axis, [((i + 1) % count, i) for i in range(ends)]),
            ],
            axis=dim,
        )
    return cells


def from_everyone(array, axis):
    size = lax.axis_size(axis)
    return lax.all_to_all(
        jnp.broadcast_to(array[None], (size, *array.shape)), axis, 0, 0, tiled=True
    )


def laid_out(tiles, dim):
    tiles = jnp.moveaxis(tiles, 0, dim)
    shape = tiles.shape
    return tiles.reshape(*shape[:dim], shape[dim] * shape[dim + 1], *shape[dim + 2 :])


def gathered_copies(array, axis, dim):
    tiles = from_everyone(array, axis)
    return laid_out(tiles, dim)


def total_of_pieces(array, axis):
    tiles = lax.all_gather(array, axis)
    return tiles.sum(axis=0)


def of_everyone(array, axis):
    return from_everyone(array, axis).sum(axis=0)


def split_up(array, dim, size):
    shape = array.shape
    tiles = array.reshape(*shape[:dim], size, shape[dim] // size, *shape[dim + 1 :])
    return jnp.moveaxis(tiles, dim, 0)


def sum_at_owner(array, axis, dim):
    size = lax.axis_size(axis)
    tiles = lax.all_to_all(split_up(array, dim, size), axis, 0, 0, tiled=True)
    return jnp.sum(tiles, axis=0)


def hankel(window, tile_rows, tile_cols):
    chans = window.shape[0]
    width = tile_rows + tile_cols
    base = window[:, : width - 1]
    tiled = jnp.broadcast_to(base[:, None, :], (chans, tile_rows, width - 1)).reshape(
        chans, tile_rows * (width - 1)
    )
    tiled = jnp.pad(tiled, ((0, 0), (0, tile_rows)))
    return tiled.reshape(chans, tile_rows, width)[:, :, :tile_cols]


def diagonal_sums(tile):
    chans, tile_rows, tile_cols = tile.shape
    width = tile_rows + tile_cols
    padded_input = jnp.pad(tile, ((0, 0), (0, 0), (0, tile_rows)))
    flat = padded_input.reshape(chans, tile_rows * width)[:, : tile_rows * (width - 1)]
    return jnp.sum(flat.reshape(chans, tile_rows, width - 1), axis=1)


def count_cells(valid_bins, offset_limit):
    sequence_length = valid_bins.shape[0]
    running = jnp.concatenate([jnp.zeros((1,), jnp.int32), jnp.cumsum(valid_bins)])
    places = jnp.arange(sequence_length, dtype=jnp.int32)
    farthest = jnp.minimum(places + offset_limit, sequence_length)
    inside = jnp.take(running, farthest) - jnp.take(running, places)
    return jnp.sum(valid_bins * inside).astype(jnp.float32)


def shards(
    encoder_in,
    gain_enc,
    conv_one,
    proj_weight,
    conv_two,
    head_weight,
    target,
    valid_bins,
    offset_limit,
    dilations,
):
    chans, encoder_bins = encoder_in.shape
    width_in = conv_one.shape[2]
    second_channels = conv_two.shape[1]
    tile_rows, tile_cols = target.shape
    area = tile_rows * tile_cols
    first_dilation = dilations[0]
    second_dilation = dilations[1]
    activ = jax.nn.gelu(gain_enc[:, None] * encoder_in.astype(jnp.float32)).astype(jnp.bfloat16)
    framed = with_halo(activ, (("enc", 1),), LARGEST_DILATION)
    channel_count = gathered_copies(framed, ("bin", "off"), 0)
    stacked_enc = jnp.concatenate(
        [
            lax.dynamic_slice_in_dim(
                channel_count,
                LARGEST_DILATION + (kernel_tap_index - 1) * first_dilation,
                encoder_bins,
                1,
            )
            for kernel_tap_index in range(3)
        ],
        axis=0,
    )
    weight_one = jnp.transpose(conv_one, (1, 0, 2)).reshape(chans, 3 * width_in)
    conv_out = jnp.dot(weight_one, stacked_enc, preferred_element_type=jnp.float32)
    hidden = (encoder_in.astype(jnp.float32) + conv_out).astype(jnp.bfloat16)
    proj_rows = jnp.transpose(proj_weight, (0, 2, 1)).reshape(2 * second_channels, chans)
    partial_embed = jnp.dot(proj_rows, hidden, preferred_element_type=jnp.float32)
    summed = total_of_pieces(partial_embed, ("bin", "off")).astype(jnp.bfloat16)
    embed = gathered_copies(summed, "enc", 1)
    sequence_length = embed.shape[1]
    window_extent = tile_cols * lax.axis_size("enc") * lax.axis_size("off")
    row_start = lax.axis_index("bin") * tile_rows
    offs_start = (lax.axis_index("enc") * lax.axis_size("off") + lax.axis_index("off")) * tile_cols
    near_rows = lax.dynamic_slice_in_dim(embed[:second_channels], row_start, tile_rows, 1)
    far_ext = jnp.concatenate(
        [embed[second_channels:], jnp.zeros((second_channels, window_extent), jnp.bfloat16)], axis=1
    )
    far_window = lax.dynamic_slice_in_dim(far_ext, row_start + offs_start, tile_rows + tile_cols, 1)
    pair_sum = near_rows[:, :, None].astype(jnp.float32) + hankel(
        far_window, tile_rows, tile_cols
    ).astype(jnp.float32)
    band_act = jnp.maximum(pair_sum, 0.0).astype(jnp.bfloat16)
    shifts = [
        (bin_displacement, offset_displacement)
        for bin_displacement in (-1, 0, 1)
        for offset_displacement in (-1, 0, 1)
    ]
    framed_band = with_halo(band_act, (("bin", 1), (("enc", "off"), 2)), LARGEST_DILATION)
    stacked_band = jnp.concatenate(
        [
            lax.dynamic_slice(
                framed_band,
                (
                    0,
                    LARGEST_DILATION + bin_displacement * second_dilation,
                    LARGEST_DILATION + offset_displacement * second_dilation,
                ),
                (second_channels, tile_rows, tile_cols),
            ).reshape(second_channels, area)
            for bin_displacement, offset_displacement in shifts
        ],
        axis=0,
    )
    weight_fwd = jnp.transpose(conv_two, (2, 0, 1)).reshape(second_channels, 9 * second_channels)
    band_conv = jnp.dot(weight_fwd, stacked_band, preferred_element_type=jnp.float32).reshape(
        second_channels, tile_rows, tile_cols
    )
    resid = pair_sum + band_conv
    prediction = jnp.sum(head_weight[:, None, None] * jnp.maximum(resid, 0.0), axis=0)
    mask_float = valid_bins.astype(jnp.float32)
    mask_ext = jnp.concatenate([mask_float, jnp.zeros((window_extent,), jnp.float32)])
    mask_near = lax.dynamic_slice_in_dim(mask_float, row_start, tile_rows)
    mask_far = hankel(
        lax.dynamic_slice_in_dim(mask_ext, row_start + offs_start, tile_rows + tile_cols)[None, :],
        tile_rows,
        tile_cols,
    )[0]
    limit_near = lax.dynamic_slice_in_dim(offset_limit, row_start, tile_rows)
    offs_ids = offs_start + jnp.arange(tile_cols, dtype=jnp.int32)
    weight = (
        mask_near[:, None]
        * mask_far
        * (offs_ids[None, :] < limit_near[:, None]).astype(jnp.float32)
    )
    denom = 1.0 + count_cells(valid_bins, offset_limit)
    differ = prediction - target.astype(jnp.float32)
    error_sum = jnp.sum(weight * differ * differ)
    dpred = 2.0 * weight * differ / denom
    dres = (head_weight[:, None, None] * dpred[None] * (resid > 0.0).astype(jnp.float32)).astype(
        jnp.bfloat16
    )
    grad_band = lax.dot_general(
        stacked_band,
        dres.reshape(second_channels, area),
        (((1,), (1,)), ((), ())),
        preferred_element_type=jnp.float32,
    ).reshape(9, second_channels, second_channels)
    framed_grad = with_halo(dres, (("bin", 1), (("enc", "off"), 2)), LARGEST_DILATION)
    stacked_grad = jnp.concatenate(
        [
            lax.dynamic_slice(
                framed_grad,
                (
                    0,
                    LARGEST_DILATION - bin_displacement * second_dilation,
                    LARGEST_DILATION - offset_displacement * second_dilation,
                ),
                (second_channels, tile_rows, tile_cols),
            ).reshape(second_channels, area)
            for bin_displacement, offset_displacement in shifts
        ],
        axis=0,
    )
    weight_back = jnp.transpose(conv_two, (1, 0, 2)).reshape(second_channels, 9 * second_channels)
    dact = jnp.dot(weight_back, stacked_grad, preferred_element_type=jnp.float32).reshape(
        second_channels, tile_rows, tile_cols
    )
    dpair = dres.astype(jnp.float32) + dact * (pair_sum > 0.0).astype(jnp.float32)
    near_grad = jnp.sum(dpair, axis=2)
    far_grad = diagonal_sums(dpair)
    enc_start = lax.axis_index("enc") * encoder_bins
    buffer = jnp.zeros((2, second_channels, sequence_length + window_extent), jnp.float32)
    buffer = lax.dynamic_update_slice(buffer, near_grad[None], (0, 0, row_start))
    buffer = lax.dynamic_update_slice(buffer, far_grad[None], (1, 0, row_start + offs_start))
    buffer = buffer[:, :, :sequence_length]
    grad_whole, grad_conv_two, total_error = lax.psum(
        (buffer, grad_band, error_sum), ("enc", "bin", "off")
    )
    grad_embed = lax.dynamic_slice_in_dim(grad_whole, enc_start, encoder_bins, 2).astype(
        jnp.bfloat16
    )
    grad_rows = grad_embed.reshape(2 * second_channels, encoder_bins)
    dhidden = jnp.dot(proj_rows.T, grad_rows, preferred_element_type=jnp.float32).astype(
        jnp.bfloat16
    )
    proj_local = jnp.dot(hidden, grad_rows.T, preferred_element_type=jnp.float32)
    proj_local = jnp.transpose(proj_local.reshape(chans, 2, second_channels), (1, 0, 2))
    conv_local = lax.dot_general(
        dhidden, stacked_enc, (((1,), (1,)), ((), ())), preferred_element_type=jnp.float32
    )
    conv_local = jnp.transpose(conv_local.reshape(chans, 3, width_in), (1, 0, 2))
    grad_proj = of_everyone(proj_local, "enc")
    grad_conv_one = sum_at_owner(conv_local, "enc", 2)
    loss_mean = (total_error / denom).reshape(1)
    return (prediction, loss_mean, grad_conv_two, grad_proj, grad_conv_one)


def solution(mesh):
    in_specs = (
        P(("bin", "off"), "enc"),
        P(("bin", "off")),
        P(None, ("bin", "off"), None),
        P(None, ("bin", "off"), None),
        P(),
        P(),
        P("bin", ("enc", "off")),
        P(),
        P(),
        P(),
    )
    out_specs = (
        P("bin", ("enc", "off")),
        P(),
        P(),
        P(None, ("bin", "off"), None),
        P(None, ("bin", "off"), "enc"),
    )
    return jax.shard_map(shards, mesh=mesh, in_specs=in_specs, out_specs=out_specs, check_vma=False)
```

profile of v0, /device:TPU:32, one launch (start us, length us, event | category | flops | bytes accessed | tf_op | source)
XLA Modules:
  0.0 812.7 jit_solution(11922956676529906253)
XLA Ops:
  18.5 5.6 all-to-all-start
  29.0 11.5 %all-to-all-done = bf16[32,16,784]{2,1,0:T(8,128)(2,1)S(1)} async-done(((bf16[32,16,784]{2,1,0:T(8,128)(2,1)}), bf16[32,16,784]{2,1,0:T(8,128)(2,1)S(1)}, u32[]{:S(2)}, u32[]{:S(2)}) %all-to-all-start) | async-done | bytes 802848 | tf_op jit(solution)/shard_map/all_to_all | solution.py:28
  44.6 91.0 %all-gather.3.cloned.1.call-done = f32[2048,768]{1,0:T(8,128)} async-done(((f32[64,768]{1,0:T(8,128)}), f32[2048,768]{1,0:T(8,128)}) %all-gather.3.cloned.1.call-update) | async-done | bytes 6291472 | tf_op jit(solution)/shard_map/all_gather | solution.py:45
  139.6 7.5 all-to-all-start.1
  147.9 34.3 %gather_fusion.1 = s32[6144]{0:T(1024)S(1)} fusion(s32[6145]{0:T(1024)S(1)} %pad_add_fusion, s32[6144]{0:T(1024)S(1)} %get-tuple-element.63), kind=kCustom, calls=%fused_computation.1.clone | custom fusion | bytes 73728 | tf_op jit(solution)/shard_map/jit(_take)/gather | solution.py:89
  182.2 34.3 %gather_fusion = s32[6144]{0:T(1024)S(1)} fusion(s32[6145]{0:T(1024)S(1)} %pad_add_fusion, s32[6144]{0:T(1024)S(1)} %get-tuple-element.64), kind=kCustom, calls=%fused_computation.clone | custom fusion | bytes 73728 | tf_op jit(solution)/shard_map/jit(_take)/gather | solution.py:89
  216.7 5.5 broadcast_in_dim.30
  222.2 21.4 %reshape.201 = bf16[32,196224]{1,0:T(8,128)(2,1)} reshape(bf16[32,384,511]{2,1,0:T(8,128)(2,1)} %broadcast_in_dim.30) | data formatting | bytes 25116672 | tf_op jit(solution)/shard_map/reshape | solution.py:69
  243.6 6.1 pad.14
  249.7 11.2 %copy.122 = bf16[4,8,384,512]{3,2,1,0:T(8,128)(2,1)S(1)} copy(bf16[4,8,384,512]{3,1,2,0:T(8,128)(2,1)S(1)} %bitcast.171) | data formatting | bytes 25165824
  261.0 4.4 copy-done.1
  299.3 10.0 %pad_reduce_fusion = f32[196608]{0:T(1024)} fusion(f32[1,196224]{1,0:T(1,128)} %broadcast_in_dim.34), kind=kLoop, calls=%fused_computation.43 | loop fusion | bytes 1571328 | tf_op jit(solution)/shard_map/jit(_pad)/pad | solution.py:72
  322.7 8.9 %pad_maximum_fusion = bf16[32,400,144]{2,1,0:T(8,128)(2,1)} fusion(bf16[32,400,8]{2,1,0:T(8,128)(2,1)} %copy.104, bf16[32,8,128]{2,1,0:T(8,128)(2,1)S(1)} %collective-permute-done.3, bf16[32,384,128]{2,1,0:T(8,128)(2,1)S(1)} %maximum_convert_fusion, bf16[32,8,128]{2,1,0:T(8,128)(2,1)} %copy-done.24, bf16[32,400,8]{2,1,0:T(8,128)(2,1)} %copy.103), kind=kLoop, calls=%fused_computation.2 | loop fusion | flops 18432000 | bytes 7372800 | tf_op jit(solution)/shard_map/concatenate | solution.py:15
  331.7 37.3 %constant_dynamic-slice_fusion.8 = (bf16[32,384,128]{2,1,0:T(8,128)(2,1)}, bf16[32,384,128]{2,1,0:T(8,128)(2,1)}, bf16[32,384,128]{2,1,0:T(8,128)(2,1)}, bf16[32...) fusion(bf16[32,400,144]{2,1,0:T(8,128)(2,1)} %pad_maximum_fusio, ...), kind=kLoop, calls=%fused_computation.89 | loop fusion | bytes 50331664 | tf_op jit(solution)/shard_map/dynamic_slice | solution.py:155
  369.0 5.5 bitcast_dynamic-update-slice_fusion.17
  403.0 11.8 %convolution_bitcast_fusion.1 = f32[4,8,384,128]{3,1,2,0:T(8,128)S(1)} fusion(bf16[288,49152]{1,0:T(8,128)(2,1)} %bitcast_dynamic-update-slice_fusion.9, bf16[32,288]{0,1:T(8,128)(2,1)S(1)} %bitcast.195), kind=kOutput, calls=%fused_computation.33 | convolution fusion | flops 905969664 | bytes 34621440 | tf_op jit(solution)/shard_map/dot_general | solution.py:169
  424.6 5.2 select_convert_fusion
  458.6 14.4 %fusion.35 = f32[9,32,32]{2,1,0:T(8,128)} fusion(bf16[9,32,49152]{2,1,0:T(8,128)(2,1)} %bitcast.26, bf16[32,49152,1]{1,0,2:T(8,128)(2,1)} %reshape.256), kind=kOutput, calls=%fused_computation.110 | convolution fusion | flops 905969664 | bytes 31494144 | tf_op jit(solution)/shard_map/dot_general | solution.py:196
  480.4 8.9 %pad_maximum_fusion.1 = bf16[32,400,144]{2,1,0:T(8,128)(2,1)} fusion(bf16[32,400,8]{2,1,0:T(8,128)(2,1)} %copy.112, bf16[32,8,128]{2,1,0:T(8,128)(2,1)S(1)} %collective-permute-done.7, bf16[32,384,128]{2,1,0:T(8,128)(2,1)S(1)} %select_convert_fusion, bf16[32,8,128]{2,1,0:T(8,128)(2,1)S(1)} %collective-permute-done.6, bf16[32,400,8]{2,1,0:T(8,128)(2,1)} %copy.111), kind=kLoop, calls=%fused_computation.3 | loop fusion | flops 18432000 | bytes 7372800 | tf_op jit(solution)/shard_map/concatenate | solution.py:15
  489.3 37.6 %constant_dynamic-slice_fusion = (bf16[32,384,128]{2,1,0:T(8,128)(2,1)}, bf16[32,384,128]{2,1,0:T(8,128)(2,1)}, bf16[32,384,128]{2,1,0:T(8,128)(2,1)}, bf16[32,3...) fusion(bf16[32,400,144]{2,1,0:T(8,128)(2,1)} %pad_maximum_fusio, ...), kind=kLoop, calls=%fused_computation.81 | loop fusion | bytes 50331664 | tf_op jit(solution)/shard_map/dynamic_slice | solution.py:205
  526.9 5.5 bitcast_dynamic-update-slice_fusion.8
  560.6 11.8 %convolution_bitcast_fusion = f32[4,8,384,128]{3,1,2,0:T(8,128)S(1)} fusion(bf16[288,49152]{1,0:T(8,128)(2,1)} %bitcast_dynamic-update-slice_fusion, bf16[32,288]{0,1:T(8,128)(2,1)S(1)} %bitcast.197), kind=kOutput, calls=%fused_computation.32 | convolution fusion | flops 905969664 | bytes 34621440 | tf_op jit(solution)/shard_map/dot_general | solution.py:219
  573.6 6.9 fusion.27
  580.4 14.4 %pad.16 = f32[32,384,512]{2,1,0:T(8,128)} pad(f32[32,384,128]{2,1,0:T(8,128)} %get-tuple-element.25, f32[]{:T(128)} %constant.90.clone.1), padding=0_0x0_0x0_384 | pad | bytes 31457284 | tf_op jit(solution)/shard_map/jit(_pad)/pad | solution.py:79
  594.8 22.0 %copy.143 = f32[4,8,384,512]{3,1,2,0:T(8,128)S(1)} copy(f32[4,8,384,512]{3,2,1,0:T(8,128)} %bitcast.164) | data formatting | bytes 50331648
  616.8 8.6 %slice.118 = f32[32,196224]{1,0:T(8,128)} slice(f32[32,196608]{1,0:T(8,128)S(1)} %bitcast.165), slice={[0:32], [0:196224]} | slice | bytes 50233344 | tf_op jit(solution)/shard_map/slice | solution.py:80
  625.4 43.9 %reshape.230 = f32[32,384,511]{2,1,0:T(8,128)} reshape(f32[32,196224]{1,0:T(8,128)} %slice.118) | data formatting | bytes 50233344 | tf_op jit(solution)/shard_map/reshape | solution.py:81
  669.3 10.0 %reduce_sum.77 = f32[32,511]{1,0:T(8,128)S(1)} reduce(f32[32,384,511]{2,1,0:T(8,128)} %reshape.230, f32[]{:T(128)} %constant.90.clone.1), dimensions={1}, to_apply=%region_9.11 | reduce | flops 6262816 | bytes 25182084 | tf_op jit(solution)/shard_map/reduce_sum | solution.py:81
  681.5 93.5 %all-reduce.7 = (f32[]{:T(128)}, f32[9,32,32]{2,1,0:T(8,128)}, bf16[2,32,6144]{2,1,0:T(8,128)(2,1)S(1)}) all-reduce(f32[]{:T(128)} %get-tuple-element.56, f32[9,32,32]{2,1,0:T(8,128)S(1)} %copy-done.25, f32[2,32,6144]{2,1,0:T(8,128)} %slice.119), channel_id=1, replica_groups=mesh['enc'=8,'bin'=16,'off'=2] {'enc','bin','off'}, use_global_device_ids=true, to_apply=%region_3.4 | all-reduce | flops 402433 | bytes 2433032 | tf_op jit(solution)/shard_map/psum | solution.py:230
  776.0 8.2 %all-to-all-start.2 = ((f32[8,1,1024]{2,1,0:T(1,128)}), f32[8,1,1024]{2,1,0:T(1,128)S(1)}, u32[]{:S(2)}, u32[]{:S(2)}) async-start(f32[8,1,1024]{2,1,0:T(1,128)} %reshape.268), calls=%async_computation.2 | async-start | bytes 65536 | tf_op jit(solution)/shard_map/all_to_all | solution.py:28
  790.7 4.7 all-to-all-start.3
  798.1 4.7 all-to-all-done.3
  (190 shorter events, 182.2 us)
Async XLA Ops:
  7.2 35.5 %copy-start.30 = (bf16[16,768]{1,0:T(8,128)(2,1)S(1)}, bf16[16,768]{1,0:T(8,128)(2,1)}, u32[]{:S(2)}) copy-start(bf16[16,768]{1,0:T(8,128)(2,1)} %param.12) | copy-start | bytes 73732
  8.2 5.8 collective-permute-start.1
  11.9 5.5 collective-permute-start
  18.5 22.0 %all-to-all-start = ((bf16[32,16,784]{2,1,0:T(8,128)(2,1)}), bf16[32,16,784]{2,1,0:T(8,128)(2,1)S(1)}, u32[]{:S(2)}, u32[]{:S(2)}) async-start(bf16[32,16,784]{2,1,0:T(8,128)(2,1)} %broadcast_in_dim.26), calls=%async_computation | async-start | bytes 1835008 | tf_op jit(solution)/shard_map/all_to_all | solution.py:28
  24.1 111.5 %all-gather.3.cloned.1.call-start = ((), (), s32[]{:S(2)}) async-start(), calls=%async_computation.4 | async-start | bytes 6488064 | tf_op jit(solution)/shard_map/all_gather | solution.py:45
  42.6 104.5 %copy-start.29 = (s32[6144]{0:T(1024)S(1)}, s32[6144]{0:T(1024)}, u32[]{:S(2)}) copy-start(s32[6144]{0:T(1024)} %param.19) | copy-start | bytes 73732
  42.6 105.2 %copy-start.26 = (s32[6144]{0:T(1024)S(1)}, s32[6144]{0:T(1024)}, u32[]{:S(2)}) copy-start(s32[6144]{0:T(1024)} %param.20) | copy-start | bytes 73732
  139.6 76.8 %all-to-all-start.1 = ((bf16[8,64,768]{2,1,0:T(8,128)(2,1)}), bf16[8,64,768]{2,1,0:T(8,128)(2,1)S(1)}, u32[]{:S(2)}, u32[]{:S(2)}) async-start(bf16[8,64,768]{2,1,0:T(8,128)(2,1)} %broadcast_in_dim.27), calls=%async_computation.1 | async-start | bytes 1572864 | tf_op jit(solution)/shard_map/all_to_all | solution.py:28
  267.4 5.1 collective-permute-start.3
  268.7 3.9 collective-permute-start.2
  280.7 34.7 %collective-permute-start.5 = (bf16[32,400,8]{1,2,0:T(8,128)(2,1)}, bf16[32,400,8]{1,2,0:T(8,128)(2,1)}, u32[]{:S(2)}, u32[]{:S(2)}) collective-permute-start(bf16[32,400,8]{1,2,0:T(8,128)(2,1)} %copy.102), channel_id=1, source_target_pairs={{1,0},{32,1},{33,32},{64,33},{65,64},{96,65},{97,96},{128,97},{129... | collective-permute-start | bytes 614408 | tf_op jit(solution)/shard_map/ppermute | solution.py:19
  287.9 31.1 %collective-permute-start.4 = (bf16[32,400,8]{1,2,0:T(8,128)(2,1)}, bf16[32,400,8]{1,2,0:T(8,128)(2,1)}, u32[]{:S(2)}, u32[]{:S(2)}) collective-permute-start(bf16[32,400,8]{1,2,0:T(8,128)(2,1)} %copy.101), channel_id=1, source_target_pairs={{0,1},{1,32},{32,33},{33,64},{64,65},{65,96},{96,97},{97,128},{128... | collective-permute-start | bytes 614408 | tf_op jit(solution)/shard_map/ppermute | solution.py:17
  369.0 9.0 %copy-start.12 = (bf16[32,384,128]{2,1,0:T(8,128)(2,1)S(1)}, bf16[32,384,128]{2,1,0:T(8,128)(2,1)}, u32[]{:S(2)}) copy-start(bf16[32,384,128]{2,1,0:T(8,128)(2,1)} %get-tuple-element.39) | copy-start | bytes 9437188
  374.5 7.1 copy-start.10
  388.6 7.4 copy-start.4
  392.0 7.5 copy-start.2
  396.0 7.0 copy-start.22
  424.6 12.6 %copy-start.23 = (bf16[9,32,32]{2,1,0:T(8,128)(2,1)S(1)}, bf16[9,32,32]{2,1,0:T(8,128)(2,1)}, u32[]{:S(2)}) copy-start(bf16[9,32,32]{2,1,0:T(8,128)(2,1)} %param.16) | copy-start | bytes 55300
  430.5 9.9 %collective-permute-start.7 = (bf16[32,8,128]{2,1,0:T(8,128)(2,1)}, bf16[32,8,128]{2,1,0:T(8,128)(2,1)S(1)}, u32[]{:S(2)}, u32[]{:S(2)}) collective-permute-start(bf16[32,8,128]{2,1,0:T(8,128)(2,1)} %get-tuple-element.47), channel_id=1, source_target_pairs={{2,0},{4,2},{6,4},{8,6},{10,8},{12,10},{14,12},{16,14},{18,16},{20... | collective-permute-start | bytes 196616 | tf_op jit(solution)/shard_map/ppermute | solution.py:19
  431.8 8.6 %collective-permute-start.6 = (bf16[32,8,128]{2,1,0:T(8,128)(2,1)}, bf16[32,8,128]{2,1,0:T(8,128)(2,1)S(1)}, u32[]{:S(2)}, u32[]{:S(2)}) collective-permute-start(bf16[32,8,128]{2,1,0:T(8,128)(2,1)} %get-tuple-element.46), channel_id=1, source_target_pairs={{0,2},{2,4},{4,6},{6,8},{8,10},{10,12},{12,14},{14,16},{16,18},{18... | collective-permute-start | bytes 196616 | tf_op jit(solution)/shard_map/ppermute | solution.py:17
  448.5 24.6 %collective-permute-start.9 = (bf16[32,400,8]{1,2,0:T(8,128)(2,1)}, bf16[32,400,8]{1,2,0:T(8,128)(2,1)}, u32[]{:S(2)}, u32[]{:S(2)}) collective-permute-start(bf16[32,400,8]{1,2,0:T(8,128)(2,1)} %copy.110), channel_id=1, source_target_pairs={{1,0},{32,1},{33,32},{64,33},{65,64},{96,65},{97,96},{128,97},{129... | collective-permute-start | bytes 614408 | tf_op jit(solution)/shard_map/ppermute | solution.py:19
  456.2 20.5 %collective-permute-start.8 = (bf16[32,400,8]{1,2,0:T(8,128)(2,1)}, bf16[32,400,8]{1,2,0:T(8,128)(2,1)}, u32[]{:S(2)}, u32[]{:S(2)}) collective-permute-start(bf16[32,400,8]{1,2,0:T(8,128)(2,1)} %copy.109), channel_id=1, source_target_pairs={{0,1},{1,32},{32,33},{33,64},{64,65},{65,96},{96,97},{97,128},{128... | collective-permute-start | bytes 614408 | tf_op jit(solution)/shard_map/ppermute | solution.py:17
  526.9 9.0 %copy-start.13 = (bf16[32,384,128]{2,1,0:T(8,128)(2,1)S(1)}, bf16[32,384,128]{2,1,0:T(8,128)(2,1)}, u32[]{:S(2)}) copy-start(bf16[32,384,128]{2,1,0:T(8,128)(2,1)} %get-tuple-element.31) | copy-start | bytes 9437188
  532.4 7.1 copy-start.11
  546.4 7.2 copy-start.5
  549.9 7.2 copy-start.3
  669.3 12.2 %copy-start.25 = (f32[9,32,32]{2,1,0:T(8,128)S(1)}, f32[9,32,32]{2,1,0:T(8,128)}, u32[]{:S(2)}) copy-start(f32[9,32,32]{2,1,0:T(8,128)} %fusion.35) | copy-start | bytes 110596
  679.3 95.7 %copy-start.28 = (bf16[16,768]{1,0:T(8,128)(2,1)S(1)}, bf16[16,768]{1,0:T(8,128)(2,1)}, u32[]{:S(2)}) copy-start(bf16[16,768]{1,0:T(8,128)(2,1)} %copy-done.27) | copy-start | bytes 73732
  679.4 104.8 %copy-start.17 = (bf16[512,768]{1,0:T(8,128)(2,1)S(1)}, bf16[512,768]{1,0:T(8,128)(2,1)}, u32[]{:S(2)}) copy-start(bf16[512,768]{1,0:T(8,128)(2,1)} %copy-done.16) | copy-start | bytes 2359300
  679.4 104.8 %copy-start.33 = (bf16[2,16,32]{2,1,0:T(8,128)(2,1)S(1)}, bf16[2,16,32]{2,1,0:T(8,128)(2,1)}, u32[]{:S(2)}) copy-start(bf16[2,16,32]{2,1,0:T(8,128)(2,1)} %param.15) | copy-start | bytes 6148
  776.0 14.7 %all-to-all-start.2 = ((f32[8,1,1024]{2,1,0:T(1,128)}), f32[8,1,1024]{2,1,0:T(1,128)S(1)}, u32[]{:S(2)}, u32[]{:S(2)}) async-start(f32[8,1,1024]{2,1,0:T(1,128)} %reshape.268), calls=%async_computation.2 | async-start | bytes 65536 | tf_op jit(solution)/shard_map/all_to_all | solution.py:28
  790.7 12.0 %all-to-all-start.3 = ((f32[8,1,3072]{2,1,0:T(1,128)}), f32[8,1,3072]{2,1,0:T(1,128)S(1)}, u32[]{:S(2)}, u32[]{:S(2)}) async-start(f32[8,1,3072]{2,1,0:T(1,128)} %reshape.270), calls=%async_computation.3 | async-start | bytes 196608 | tf_op jit(solution)/shard_map/all_to_all | solution.py:61
  (19 other events, 82.5 us)
Sparse Core Ops, SparseCore 0:
  44.8 90.7 all-gather.2
where the time goes:
time: 823 us; the launch traced here: 813 us
  local copies, waits for them, and re-layouts  430 us (52%)
  waiting for transfers between devices  114 us (14%)
  blocking collectives  93.5 us (11%)
  other arithmetic  56 us (7%)
  starting transfers between devices  53.5 us (7%)
  matrix products  41.6 us (5%)
  between operations  24 us (3%)
    unnamed x100, local copies, waits for them, and re-layouts  109 us
    psum x1, blocking collectives, shards(): lax.psum((buffer, grad_band, error_sum), ('enc', 'bin', 'off'))  93.5 us
    all_gather x1, waiting for transfers between devices, total_of_pieces(): tiles = lax.all_gather(array, axis)  91 us
    gather x2, local copies, waits for them, and re-layouts, count_cells(): inside = jnp.take(running, farthest) - jnp.take(running, places)  68.6 us
    reshape x1, local copies, waits for them, and re-layouts, diagonal_sums(): return jnp.sum(flat.reshape(chans, tile_rows, width - 1), axis=1)  43.9 us
    dynamic_slice x1, local copies, waits for them, and re-layouts, shards(): lax.dynamic_slice(framed_grad, (0, LARGEST_DILATION - bin_displacement *...  37.6 us
    dynamic_slice x1, local copies, waits for them, and re-layouts, shards(): lax.dynamic_slice(framed_band, (0, LARGEST_DILATION + bin_displacement *...  37.3 us
    reshape x1, local copies, waits for them, and re-layouts, hankel(): jnp.broadcast_to(base[:, None, :], (chans, tile_rows, width - 1))  21.4 us
  transfers between devices with their start and end apart: 15, of which 6 were waited for; matrix products, arithmetic and copies ran while one was open for 16% of the time, Pallas kernels for 0%

commit v1 on v0

--- a/solution.py
+++ b/solution.py
@@ -4,6 +4,11 @@
 from jax.sharding import PartitionSpec as P
 
 LARGEST_DILATION = 8
+
+
+def by_each_axis(array_2, inner_axis, outer_axis):
+    half = lax.psum(array_2, inner_axis)
+    return lax.psum(half, outer_axis)
 
 
 def with_halo(cells, sides, width):
@@ -227,8 +232,8 @@
     buffer = lax.dynamic_update_slice(buffer, near_grad[None], (0, 0, row_start))
     buffer = lax.dynamic_update_slice(buffer, far_grad[None], (1, 0, row_start + offs_start))
     buffer = buffer[:, :, :sequence_length]
-    grad_whole, grad_conv_two, total_error = lax.psum(
-        (buffer, grad_band, error_sum), ("enc", "bin", "off")
+    grad_whole, grad_conv_two, total_error = by_each_axis(
+        (buffer, grad_band, error_sum), ("bin", "off"), "enc"
     )
     grad_embed = lax.dynamic_slice_in_dim(grad_whole, enc_start, encoder_bins, 2).astype(
         jnp.bfloat16

time: 823 us -> 926 us (1.13)
  blocking collectives: 93.5 us -> 199 us
    psum x1 -> x2, blocking collectives: 93.5 us -> 199 us  [the longest x1 133 us: by_each_axis(): half = lax.psum(array_2, inner_axis)]
    unnamed x100 -> x102, local copies, waits for them, and re-layouts: 109 us -> 109 us
  transfers between devices with their start and end apart: 15 -> 16, of which waited for: 6 -> 7; matrix products, arithmetic and copies ran while one was open for 16% -> 14% of each run, Pallas kernels for 0% -> 0%
where the time goes in v1:
time: 926 us; the launch traced here: 915 us
  local copies, waits for them, and re-layouts  430 us (46%)
  blocking collectives  199 us (21%)
  waiting for transfers between devices  116 us (13%)
  other arithmetic  55.8 us (6%)
  starting transfers between devices  50.7 us (5%)
  matrix products  39.4 us (4%)
  between operations  23.9 us (3%)
    psum x1, blocking collectives, by_each_axis(): half = lax.psum(array_2, inner_axis)  133 us
    unnamed x102, local copies, waits for them, and re-layouts  109 us
    all_gather x1, waiting for transfers between devices, total_of_pieces(): tiles = lax.all_gather(array, axis)  91 us
    gather x2, local copies, waits for them, and re-layouts, count_cells(): inside = jnp.take(running, farthest) - jnp.take(running, places)  68.6 us
    psum x1, blocking collectives, by_each_axis(): return lax.psum(half, outer_axis)  66.4 us
    reshape x1, local copies, waits for them, and re-layouts, diagonal_sums(): return jnp.sum(flat.reshape(chans, tile_rows, width - 1), axis=1)  43.9 us
    dynamic_slice x1, local copies, waits for them, and re-layouts, shards(): lax.dynamic_slice(framed_band, (0, LARGEST_DILATION + bin_displacement *...  37.8 us
    dynamic_slice x1, local copies, waits for them, and re-layouts, shards(): lax.dynamic_slice(framed_grad, (0, LARGEST_DILATION - bin_displacement *...  37 us
  transfers between devices with their start and end apart: 16, of which 7 were waited for; matrix products, arithmetic and copies ran while one was open for 14% of the time, Pallas kernels for 0%

profile of v1, /device:TPU:32, one launch (start us, length us, event | category | flops | bytes accessed | tf_op | source)
XLA Modules:
  0.0 915.1 jit_solution(6404339085741249478)
XLA Ops:
  18.5 5.6 all-to-all-start
  29.0 11.5 %all-to-all-done = bf16[32,16,784]{2,1,0:T(8,128)(2,1)S(1)} async-done(((bf16[32,16,784]{2,1,0:T(8,128)(2,1)}), bf16[32,16,784]{2,1,0:T(8,128)(2,1)S(1)}, u32[]{:S(2)}, u32[]{:S(2)}) %all-to-all-start) | async-done | bytes 802848 | tf_op jit(solution)/shard_map/all_to_all | solution.py:33
  44.7 91.0 %all-gather.3.cloned.1.call-done = f32[2048,768]{1,0:T(8,128)} async-done(((f32[64,768]{1,0:T(8,128)}), f32[2048,768]{1,0:T(8,128)}) %all-gather.3.cloned.1.call-update) | async-done | bytes 6291472 | tf_op jit(solution)/shard_map/all_gather | solution.py:50
  139.7 7.5 all-to-all-start.1
  147.9 34.3 %gather_fusion.1 = s32[6144]{0:T(1024)S(1)} fusion(s32[6145]{0:T(1024)S(1)} %pad_add_fusion, s32[6144]{0:T(1024)S(1)} %get-tuple-element.65), kind=kCustom, calls=%fused_computation.1.clone | custom fusion | bytes 73728 | tf_op jit(solution)/shard_map/jit(_take)/gather | solution.py:94
  182.2 34.3 %gather_fusion = s32[6144]{0:T(1024)S(1)} fusion(s32[6145]{0:T(1024)S(1)} %pad_add_fusion, s32[6144]{0:T(1024)S(1)} %get-tuple-element.66), kind=kCustom, calls=%fused_computation.clone | custom fusion | bytes 73728 | tf_op jit(solution)/shard_map/jit(_take)/gather | solution.py:94
  216.7 5.6 broadcast_in_dim.30
  222.3 21.4 %reshape.201 = bf16[32,196224]{1,0:T(8,128)(2,1)} reshape(bf16[32,384,511]{2,1,0:T(8,128)(2,1)} %broadcast_in_dim.30) | data formatting | bytes 25116672 | tf_op jit(solution)/shard_map/reshape | solution.py:74
  243.7 6.1 pad.14
  249.8 11.2 %copy.122 = bf16[4,8,384,512]{3,2,1,0:T(8,128)(2,1)S(1)} copy(bf16[4,8,384,512]{3,1,2,0:T(8,128)(2,1)S(1)} %bitcast.171) | data formatting | bytes 25165824
  299.5 10.0 %pad_reduce_fusion = f32[196608]{0:T(1024)} fusion(f32[1,196224]{1,0:T(1,128)} %broadcast_in_dim.34), kind=kLoop, calls=%fused_computation.43 | loop fusion | bytes 1571328 | tf_op jit(solution)/shard_map/jit(_pad)/pad | solution.py:77
  323.1 8.9 pad_maximum_fusion
  332.0 37.8 %constant_dynamic-slice_fusion.8 = (bf16[32,384,128]{2,1,0:T(8,128)(2,1)}, bf16[32,384,128]{2,1,0:T(8,128)(2,1)}, bf16[32,384,128]{2,1,0:T(8,128)(2,1)}, bf16[32...) fusion(bf16[32,400,144]{2,1,0:T(8,128)(2,1)} %pad_maximum_fusio, ...), kind=kLoop, calls=%fused_computation.89 | loop fusion | bytes 50331664 | tf_op jit(solution)/shard_map/dynamic_slice | solution.py:160
  369.8 5.5 bitcast_dynamic-update-slice_fusion.17
  403.8 11.8 %convolution_bitcast_fusion.1 = f32[4,8,384,128]{3,1,2,0:T(8,128)S(1)} fusion(bf16[288,49152]{1,0:T(8,128)(2,1)} %bitcast_dynamic-update-slice_fusion.9, bf16[32,288]{0,1:T(8,128)(2,1)S(1)} %bitcast.195), kind=kOutput, calls=%fused_computation.33 | convolution fusion | flops 905969664 | bytes 34621440 | tf_op jit(solution)/shard_map/dot_general | solution.py:174
  425.2 5.2 select_convert_fusion
  466.8 8.8 pad_maximum_fusion.1
  475.6 37.0 %constant_dynamic-slice_fusion = (bf16[32,384,128]{2,1,0:T(8,128)(2,1)}, bf16[32,384,128]{2,1,0:T(8,128)(2,1)}, bf16[32,384,128]{2,1,0:T(8,128)(2,1)}, bf16[32,3...) fusion(bf16[32,400,144]{2,1,0:T(8,128)(2,1)} %pad_maximum_fusio, ...), kind=kLoop, calls=%fused_computation.81 | loop fusion | bytes 50331664 | tf_op jit(solution)/shard_map/dynamic_slice | solution.py:210
  512.6 5.5 bitcast_dynamic-update-slice_fusion.8
  546.4 11.8 %convolution_bitcast_fusion = f32[4,8,384,128]{3,1,2,0:T(8,128)S(1)} fusion(bf16[288,49152]{1,0:T(8,128)(2,1)} %bitcast_dynamic-update-slice_fusion, bf16[32,288]{0,1:T(8,128)(2,1)S(1)} %bitcast.197), kind=kOutput, calls=%fused_computation.32 | convolution fusion | flops 905969664 | bytes 34621440 | tf_op jit(solution)/shard_map/dot_general | solution.py:224
  559.4 6.8 fusion.27
  566.2 14.4 %pad.16 = f32[32,384,512]{2,1,0:T(8,128)} pad(f32[32,384,128]{2,1,0:T(8,128)} %get-tuple-element.27, f32[]{:T(128)} %constant.90.clone.1), padding=0_0x0_0x0_384 | pad | bytes 31457284 | tf_op jit(solution)/shard_map/jit(_pad)/pad | solution.py:84
  580.6 21.9 %copy.143 = f32[4,8,384,512]{3,1,2,0:T(8,128)S(1)} copy(f32[4,8,384,512]{3,2,1,0:T(8,128)} %bitcast.164) | data formatting | bytes 50331648
  602.6 8.6 slice.118
  611.2 43.9 %reshape.230 = f32[32,384,511]{2,1,0:T(8,128)} reshape(f32[32,196224]{1,0:T(8,128)} %slice.118) | data formatting | bytes 50233344 | tf_op jit(solution)/shard_map/reshape | solution.py:86
  655.1 10.0 %reduce_sum.77 = f32[32,511]{1,0:T(8,128)S(1)} reduce(f32[32,384,511]{2,1,0:T(8,128)} %reshape.230, f32[]{:T(128)} %constant.90.clone.1), dimensions={1}, to_apply=%region_11.13 | reduce | flops 6262816 | bytes 25182084 | tf_op jit(solution)/shard_map/reduce_sum | solution.py:86
  667.3 13.6 %fusion.35 = f32[9,32,32]{2,1,0:T(8,128)S(1)} fusion(bf16[9,32,49152]{2,1,0:T(8,128)(2,1)} %bitcast.26, bf16[32,49152,1]{1,0,2:T(8,128)(2,1)} %reshape.256), kind=kOutput, calls=%fused_computation.110 | convolution fusion | flops 905969664 | bytes 31494144 | tf_op jit(solution)/shard_map/dot_general | solution.py:201
  680.9 133.0 %all-reduce.5 = (f32[]{:T(128)}, f32[9,32,32]{2,1,0:T(8,128)S(1)}) all-reduce(f32[]{:T(128)} %get-tuple-element.58, f32[9,32,32]{2,1,0:T(8,128)S(1)} %fusion.35), channel_id=1, replica_groups=mesh['enc'=8,'bin'=16,'off'=2] {'bin','off'}, use_global_device_ids=true, to_apply=%region_3.4 | all-reduce | flops 9217 | bytes 73736 | tf_op jit(solution)/shard_map/psum | solution.py:10
  814.0 66.4 %all-reduce.11 = (f32[]{:T(128)}, f32[9,32,32]{2,1,0:T(8,128)}, bf16[2,32,6144]{2,1,0:T(8,128)(2,1)S(1)}) all-reduce(f32[]{:T(128)} %get-tuple-element.21, f32[9,32,32]{2,1,0:T(8,128)S(1)} %get-tuple-element.22, f32[2,32,6144]{2,1,0:T(8,128)} %all-reduce.10.cloned.1.call-done), channel_id=1, replica_groups=mesh['enc'=8,'bin'=16,'off'=2] {'enc'}, use_global_device_ids=true, to_apply=%region_4.5 | all-reduce | flops 402433 | bytes 2433032 | tf_op jit(solution)/shard_map/psum | solution.py:11
  881.3 5.4 all-to-all-start.2
  893.3 4.7 all-to-all-start.3
  900.6 4.7 all-to-all-done.3
  (196 shorter events, 186.9 us)
Async XLA Ops:
  7.2 35.4 %copy-start.31 = (bf16[16,768]{1,0:T(8,128)(2,1)S(1)}, bf16[16,768]{1,0:T(8,128)(2,1)}, u32[]{:S(2)}) copy-start(bf16[16,768]{1,0:T(8,128)(2,1)} %param.12) | copy-start | bytes 73732
  8.2 5.8 collective-permute-start.1
  11.9 5.5 collective-permute-start
  18.5 22.0 %all-to-all-start = ((bf16[32,16,784]{2,1,0:T(8,128)(2,1)}), bf16[32,16,784]{2,1,0:T(8,128)(2,1)S(1)}, u32[]{:S(2)}, u32[]{:S(2)}) async-start(bf16[32,16,784]{2,1,0:T(8,128)(2,1)} %broadcast_in_dim.26), calls=%async_computation | async-start | bytes 1835008 | tf_op jit(solution)/shard_map/all_to_all | solution.py:33
  24.1 111.5 %all-gather.3.cloned.1.call-start = ((), (), s32[]{:S(2)}) async-start(), calls=%async_computation.5 | async-start | bytes 6488064 | tf_op jit(solution)/shard_map/all_gather | solution.py:50
  42.6 104.6 %copy-start.30 = (s32[6144]{0:T(1024)S(1)}, s32[6144]{0:T(1024)}, u32[]{:S(2)}) copy-start(s32[6144]{0:T(1024)} %param.19) | copy-start | bytes 73732
  42.6 105.3 %copy-start.27 = (s32[6144]{0:T(1024)S(1)}, s32[6144]{0:T(1024)}, u32[]{:S(2)}) copy-start(s32[6144]{0:T(1024)} %param.20) | copy-start | bytes 73732
  139.7 76.8 %all-to-all-start.1 = ((bf16[8,64,768]{2,1,0:T(8,128)(2,1)}), bf16[8,64,768]{2,1,0:T(8,128)(2,1)S(1)}, u32[]{:S(2)}, u32[]{:S(2)}) async-start(bf16[8,64,768]{2,1,0:T(8,128)(2,1)} %broadcast_in_dim.27), calls=%async_computation.1 | async-start | bytes 1572864 | tf_op jit(solution)/shard_map/all_to_all | solution.py:33
  147.2 666.8 %all-reduce.10.cloned.1.call-start = ((), (), s32[]{:S(2)}) async-start(), calls=%async_computation.4 | async-start | bytes 3145728 | tf_op jit(solution)/shard_map/psum | solution.py:10
  267.6 5.1 collective-permute-start.3
  268.9 3.9 collective-permute-start.2
  280.9 34.8 %collective-permute-start.5 = (bf16[32,400,8]{1,2,0:T(8,128)(2,1)}, bf16[32,400,8]{1,2,0:T(8,128)(2,1)}, u32[]{:S(2)}, u32[]{:S(2)}) collective-permute-start(bf16[32,400,8]{1,2,0:T(8,128)(2,1)} %copy.102), channel_id=1, source_target_pairs={{1,0},{32,1},{33,32},{64,33},{65,64},{96,65},{97,96},{128,97},{129... | collective-permute-start | bytes 614408 | tf_op jit(solution)/shard_map/ppermute | solution.py:24
  288.2 31.1 %collective-permute-start.4 = (bf16[32,400,8]{1,2,0:T(8,128)(2,1)}, bf16[32,400,8]{1,2,0:T(8,128)(2,1)}, u32[]{:S(2)}, u32[]{:S(2)}) collective-permute-start(bf16[32,400,8]{1,2,0:T(8,128)(2,1)} %copy.101), channel_id=1, source_target_pairs={{0,1},{1,32},{32,33},{33,64},{64,65},{65,96},{96,97},{97,128},{128... | collective-permute-start | bytes 614408 | tf_op jit(solution)/shard_map/ppermute | solution.py:22
  369.8 9.0 copy-start.12
  382.3 7.2 copy-start.8
  389.4 7.4 copy-start.4
  392.9 7.4 copy-start.2
  430.5 4.8 collective-permute-start.7
  431.8 4.4 collective-permute-start.6
  440.2 16.3 %copy-start.25 = (bf16[9,32,32]{2,1,0:T(8,128)(2,1)S(1)}, bf16[9,32,32]{2,1,0:T(8,128)(2,1)}, u32[]{:S(2)}) copy-start(bf16[9,32,32]{2,1,0:T(8,128)(2,1)} %param.16) | copy-start | bytes 55300
  444.3 15.1 %collective-permute-start.9 = (bf16[32,400,8]{1,2,0:T(8,128)(2,1)}, bf16[32,400,8]{1,2,0:T(8,128)(2,1)}, u32[]{:S(2)}, u32[]{:S(2)}) collective-permute-start(bf16[32,400,8]{1,2,0:T(8,128)(2,1)} %copy.110), channel_id=1, source_target_pairs={{1,0},{32,1},{33,32},{64,33},{65,64},{96,65},{97,96},{128,97},{129... | collective-permute-start | bytes 614408 | tf_op jit(solution)/shard_map/ppermute | solution.py:24
  452.1 10.9 %collective-permute-start.8 = (bf16[32,400,8]{1,2,0:T(8,128)(2,1)}, bf16[32,400,8]{1,2,0:T(8,128)(2,1)}, u32[]{:S(2)}, u32[]{:S(2)}) collective-permute-start(bf16[32,400,8]{1,2,0:T(8,128)(2,1)} %copy.109), channel_id=1, source_target_pairs={{0,1},{1,32},{32,33},{33,64},{64,65},{65,96},{96,97},{97,128},{128... | collective-permute-start | bytes 614408 | tf_op jit(solution)/shard_map/ppermute | solution.py:22
  512.6 9.0 copy-start.13
  532.0 7.5 copy-start.5
  535.5 7.5 copy-start.3
  667.3 213.1 %copy-start.29 = (bf16[16,768]{1,0:T(8,128)(2,1)S(1)}, bf16[16,768]{1,0:T(8,128)(2,1)}, u32[]{:S(2)}) copy-start(bf16[16,768]{1,0:T(8,128)(2,1)} %copy-done.28) | copy-start | bytes 73732
  667.3 219.5 %copy-start.17 = (bf16[512,768]{1,0:T(8,128)(2,1)S(1)}, bf16[512,768]{1,0:T(8,128)(2,1)}, u32[]{:S(2)}) copy-start(bf16[512,768]{1,0:T(8,128)(2,1)} %copy-done.16) | copy-start | bytes 2359300
  667.3 219.5 %copy-start.19 = (bf16[512,768]{1,0:T(8,128)(2,1)S(1)}, bf16[512,768]{1,0:T(8,128)(2,1)}, u32[]{:S(2)}) copy-start(bf16[512,768]{1,0:T(8,128)(2,1)} %copy-done.18) | copy-start | bytes 2359300
  667.3 219.5 %copy-start.21 = (bf16[512,768]{1,0:T(8,128)(2,1)S(1)}, bf16[512,768]{1,0:T(8,128)(2,1)}, u32[]{:S(2)}) copy-start(bf16[512,768]{1,0:T(8,128)(2,1)} %copy-done.20) | copy-start | bytes 2359300
  667.3 219.5 %copy-start.34 = (bf16[2,16,32]{2,1,0:T(8,128)(2,1)S(1)}, bf16[2,16,32]{2,1,0:T(8,128)(2,1)}, u32[]{:S(2)}) copy-start(bf16[2,16,32]{2,1,0:T(8,128)(2,1)} %param.15) | copy-start | bytes 6148
  881.3 12.0 %all-to-all-start.2 = ((f32[8,1,1024]{2,1,0:T(1,128)}), f32[8,1,1024]{2,1,0:T(1,128)S(1)}, u32[]{:S(2)}, u32[]{:S(2)}) async-start(f32[8,1,1024]{2,1,0:T(1,128)} %reshape.268), calls=%async_computation.2 | async-start | bytes 65536 | tf_op jit(solution)/shard_map/all_to_all | solution.py:33
  893.3 12.0 %all-to-all-start.3 = ((f32[8,1,3072]{2,1,0:T(1,128)}), f32[8,1,3072]{2,1,0:T(1,128)S(1)}, u32[]{:S(2)}, u32[]{:S(2)}) async-start(f32[8,1,3072]{2,1,0:T(1,128)} %reshape.270), calls=%async_computation.3 | async-start | bytes 196608 | tf_op jit(solution)/shard_map/all_to_all | solution.py:66
  (21 other events, 96.2 us)
Sparse Core Ops, SparseCore 0:
  44.8 90.7 all-gather.2
  667.4 130.9 all-reduce.9
